TPU v7x, 32 devices: a whole 2x2x4 slice. The times are simulated.
32 devices in a mesh: ep: 32 (over z, y, x, core).
Axes of the slice: x: 2, y: 2, z: 4, core: 2. Of those that a mesh axis runs over, the one named last changes fastest.
Arguments:
- tokens: bfloat16 [512, 7168], P('ep'), may hold values from -6 to 6
- router_weight: bfloat16 [7168, 16], replicated, may hold values from -0.0625 to 0.0625
- expert_ids: int32 [512, 8], P('ep'), may hold values from 0 to 15, as said below
- gate_proj: bfloat16 [32, 2, 7168, 256], P('ep'), may hold values from -0.0625 to 0.0625
- up_proj: bfloat16 [32, 2, 7168, 256], P('ep'), may hold values from -0.0625 to 0.0625
- down_proj: bfloat16 [32, 2, 256, 7168], P('ep'), may hold values from -0.1875 to 0.1875
Outputs:
- mixed: bfloat16 [512, 7168], P('ep')
- load_excess: float32 [16], replicated
Inputs may be any that keep to these rules, and one draw needn't show every extreme that they name: `expert_ids`: each token names 8 different experts, all in different groups (expert e is in group e // 2). Among the 16 tokens of any one index of ep, at most 16 choices name experts of any one group, and some group is named by exactly 16 of them.
All inputs are finite; a program needn't handle non-finite values.
Results may differ from a plain program's by a relative error of at most 0.015.
Values may be sent and summed in bfloat16 or wider, within the bound.
A program may use at most 128 MiB of HBM per device.

v0:
```python
import jax
import jax.numpy as jnp
from jax import lax
from jax.sharding import PartitionSpec as P

SPLIT = 4


route_scale = 2.5


def per_device(tokens, router_weight, expert_ids, gate_proj, up_proj, down_proj):
    device_count = lax.axis_size("ep")
    group_count = device_count // SPLIT
    tok_rows, fanout = expert_ids.shape
    features = tokens.shape[1]
    experts = router_weight.shape[1]
    held_experts = gate_proj.shape[1]
    assigned = tok_rows * fanout
    capacity = max(2, (assigned + group_count - 1) // group_count)
    logits = jnp.dot(tokens, router_weight, preferred_element_type=jnp.float32)
    scores = jax.nn.sigmoid(logits)
    picked = jnp.take_along_axis(scores, expert_ids, axis=1)
    gate_weights = route_scale * picked / jnp.sum(picked, axis=1, keepdims=True)
    chosen = expert_ids.reshape(-1)
    one_hot = (chosen[:, None] == jnp.arange(experts, dtype=jnp.int32)[None, :]).astype(jnp.int32)
    sent_counts = jnp.sum(one_hot, axis=0)
    earlier = jnp.cumsum(one_hot, axis=0) - one_hot
    order_rank = jnp.take_along_axis(earlier, chosen[:, None], axis=1)[:, 0]
    group_counts = sent_counts.reshape(group_count, held_experts)
    before = (jnp.cumsum(group_counts, axis=1) - group_counts).reshape(-1)
    slot_index = chosen // held_experts * capacity + before[chosen] + order_rank
    owners = jnp.arange(assigned, dtype=jnp.int32) // fanout
    group_rows = (
        jnp.zeros((group_count * capacity, features), tokens.dtype)
        .at[slot_index]
        .set(tokens[owners])
    )
    group_rows = group_rows.reshape(group_count, 1, capacity, features)
    send_rows = jnp.broadcast_to(group_rows, (group_count, SPLIT, capacity, features)).reshape(
        device_count, capacity, features
    )
    peer_counts = jnp.broadcast_to(
        group_counts[:, None, :], (group_count, SPLIT, held_experts)
    ).reshape(device_count, held_experts)
    arrived_counts = lax.all_to_all(peer_counts, "ep", split_axis=0, concat_axis=0, tiled=True)
    arrived = lax.all_to_all(send_rows, "ep", split_axis=0, concat_axis=0, tiled=True)
    quarter = lax.axis_index("ep") % SPLIT
    senders = jnp.arange(device_count, dtype=jnp.int32)
    mine = (senders % SPLIT == quarter)[:, None]
    own_loads = jnp.sum(jnp.where(mine, arrived_counts, 0), axis=0)
    gathered = lax.all_gather(own_loads, "ep", axis=0, tiled=True)
    expert_loads = (
        jnp.sum(gathered.reshape(group_count, SPLIT, held_experts), axis=1)
        .reshape(-1)
        .astype(jnp.float32)
    )
    load_excess = expert_loads - float(assigned * SPLIT // held_experts)
    arrived_rows = arrived.reshape(device_count * capacity, features)
    bounds = jnp.cumsum(arrived_counts, axis=1)
    position = jnp.arange(capacity, dtype=jnp.int32)
    local_expert = jnp.sum(
        (position[None, :, None] >= bounds[:, None, :]).astype(jnp.int32), axis=2
    ).reshape(-1)
    gate_act = jnp.einsum(
        "rd,edf->erf", arrived_rows, gate_proj[0], preferred_element_type=jnp.float32
    )
    up_act = jnp.einsum("rd,edf->erf", arrived_rows, up_proj[0], preferred_element_type=jnp.float32)
    hidden = (jax.nn.silu(gate_act) * up_act).astype(jnp.bfloat16)
    produced = jnp.einsum("erf,efd->erd", hidden, down_proj[0], preferred_element_type=jnp.float32)
    result = jnp.zeros((device_count * capacity, features), jnp.float32)
    for slot_expert in range(held_experts):
        result = jnp.where((local_expert == slot_expert)[:, None], produced[slot_expert], result)
    returned = lax.all_to_all(
        result.reshape(device_count, capacity, features).astype(jnp.bfloat16),
        "ep",
        split_axis=0,
        concat_axis=0,
        tiled=True,
    ).astype(jnp.float32)
    expert_out = jnp.sum(returned.reshape(group_count, SPLIT, capacity, features), axis=1).astype(
        jnp.bfloat16
    )
    own_rows = expert_out.reshape(group_count * capacity, features)[slot_index].reshape(
        tok_rows, fanout, features
    )
    combined = jnp.einsum(
        "tk,tkd->td", gate_weights, own_rows.astype(jnp.float32), preferred_element_type=jnp.float32
    )
    return (combined.astype(jnp.bfloat16), load_excess)


def solution(mesh):
    in_specs = (
        P("ep", None),
        P(),
        P("ep", None),
        P("ep", None, None, None),
        P("ep", None, None, None),
        P("ep", None, None, None),
    )
    out_specs = (P("ep", None), P())
    return jax.shard_map(
        per_device, mesh=mesh, in_specs=in_specs, out_specs=out_specs, check_vma=False
    )
```

profile of v0, /device:TPU:0, one launch (start us, length us, event | category | flops | bytes accessed | tf_op | source)
XLA Modules:
  0.0 451.2 jit_solution(14168166099956182927)
XLA Ops:
  0.6 0.8 copy.33
  2.0 0.6 broadcast_in_dim.66.clone
  2.6 7.4 %all-to-all-start = ((s32[32,1,2]{2,1,0:T(1,128)}), s32[32,1,2]{2,1,0:T(1,128)S(1)}, u32[]{:S(2)}, u32[]{:S(2)}) async-start(s32[32,1,2]{2,1,0:T(1,128)} %bitcast.2), calls=%async_computation | async-start | bytes 32768 | tf_op jit(solution)/shard_map/all_to_all | solution.py:46
  10.4 0.7 fusion.38
  11.2 1.3 gather_fusion.2
  12.4 10.0 %fusion.35 = s32[128]{0:T(128)S(1)} fusion(s32[128]{0:T(128)S(1)} %gather_fusion.2, s32[128,1]{0,1:T(1,128)S(1)} %reshape.354, s32[]{:T(128)} %bitcast.22, s32[]{:T(128)} %bitcast.23, s32[]{:T(128)} %bitcast.24, s32[]{:T(128)} %bitcast.25, s32[]{:T(128)} %bitcast.26, s32[]{:T(128)} %bitcast.28, s32[]{:T(128)} %bitcast.27, s32[]{:T(128)} %bitcast.5, ...), kind=kLoop, calls=%fused_computation.79 | loop fusion | flops 7296 | bytes 1600 | tf_op jit(solution)/shard_map/select_n | solution.py:37
  22.4 8.8 %scatter_custom_fusion = bf16[128,7168]{1,0:T(8,128)(2,1)S(1)} fusion(s32[128]{0:T(128)S(1)} %fusion.35, bf16[16,7168]{1,0:T(8,128)(2,1)S(1)} %copy-done, s32[1024]{0:T(1024)S(1)} %pad_clamp_fusion.1, bf16[]{:T(256)} %constant.100.clone.1), kind=kCustom, calls=%fused_computation.15 | custom fusion | bytes 1835010 | tf_op jit(solution)/shard_map/scatter | solution.py:37
  31.2 4.1 broadcast_in_dim.71
  35.3 6.1 %all-to-all-start.1 = ((bf16[32,16,7168]{2,1,0:T(8,128)(2,1)}), bf16[32,16,7168]{2,1,0:T(8,128)(2,1)}, u32[]{:S(2)}, u32[]{:S(2)}) async-start(bf16[32,16,7168]{2,1,0:T(8,128)(2,1)} %bitcast.213), calls=%async_computation.1 | async-start | bytes 14680064 | tf_op jit(solution)/shard_map/all_to_all | solution.py:47
  41.7 153.5 %all-to-all-done.1 = bf16[32,16,7168]{2,1,0:T(8,128)(2,1)} async-done(((bf16[32,16,7168]{2,1,0:T(8,128)(2,1)}), bf16[32,16,7168]{2,1,0:T(8,128)(2,1)}, u32[]{:S(2)}, u32[]{:S(2)}) %all-to-all-start.1) | async-done | bytes 7340064 | tf_op jit(solution)/shard_map/all_to_all | solution.py:47
  195.3 8.4 %fusion.10 = f32[2,512,256]{2,1,0:T(8,128)S(1)} fusion(bf16[512,7168,1]{1,0,2:T(8,128)(2,1)} %bitcast.39, bf16[1,2,7168,256]{3,2,1,0:T(8,128)(2,1)} %param.9), kind=kOutput, calls=%fused_computation.17 | convolution fusion | flops 3758096384 | bytes 15728640 | tf_op jit(solution)/shard_map/rd,edf->erf/dot_general | solution.py:65
  203.6 9.2 %fusion.19 = bf16[2,512,256]{2,1,0:T(8,128)(2,1)S(1)} fusion(bf16[512,7168,1]{1,0,2:T(8,128)(2,1)} %bitcast.39, bf16[1,2,7168,256]{3,2,1,0:T(8,128)(2,1)} %param.10, f32[2,512,256]{2,1,0:T(8,128)S(1)} %fusion.10), kind=kOutput, calls=%fused_computation.20 | convolution fusion | flops 3759669248 | bytes 16252928 | tf_op jit(solution)/shard_map/rd,edf->erf/dot_general | solution.py:68
  212.9 10.5 %fusion = bf16[2,512,7168]{2,1,0:T(8,128)(2,1)} fusion(bf16[2,512,256]{2,1,0:T(8,128)(2,1)S(1)} %fusion.19, bf16[1,2,256,7168]{3,2,1,0:T(8,128)(2,1)} %param.11), kind=kOutput, calls=%fused_computation.7 | convolution fusion | flops 3758096384 | bytes 22544384 | tf_op jit(solution)/shard_map/erf,efd->erd/dot_general | solution.py:70
  223.3 10.4 %fusion.37 = (bf16[1,512,7168]{2,1,0:T(8,128)(2,1)}, bf16[1,512,7168]{2,1,0:T(8,128)(2,1)}) fusion(bf16[2,512,7168]{2,1,0:T(8,128)(2,1)} %fusion), kind=kLoop, calls=%fused_computation.82 | loop fusion | bytes 29360128 | tf_op jit(solution)/shard_map/slice | solution.py:73
  233.7 13.3 %select_convert_fusion = bf16[32,16,7168]{2,1,0:T(8,128)(2,1)} fusion(bf16[32,16,7168]{2,1,0:T(8,128)(2,1)} %bitcast.212, bf16[32,16,7168]{2,1,0:T(8,128)(2,1)} %bitcast.211, pred[32,16]{1,0:T(8,128)(4,1)S(1)} %copy.40, pred[32,16]{1,0:T(8,128)(4,1)S(1)} %copy.37), kind=kLoop, calls=%fused_computation.5 | loop fusion | flops 7340032 | bytes 22021120 | tf_op jit(solution)/shard_map/convert_element_type | solution.py:75
  247.0 11.5 %all-to-all-start.2 = ((bf16[32,16,7168]{2,1,0:T(8,128)(2,1)}), bf16[32,16,7168]{2,1,0:T(8,128)(2,1)}, u32[]{:S(2)}, u32[]{:S(2)}) async-start(bf16[32,16,7168]{2,1,0:T(8,128)(2,1)} %select_convert_fusion), calls=%async_computation.2 | async-start | bytes 14680064 | tf_op jit(solution)/shard_map/all_to_all | solution.py:74
  258.9 1.3 gather_fusion.1
  260.7 0.2 dynamic-update-slice
  260.9 179.1 %all-reduce = s32[64]{0:T(128)S(1)} all-reduce(s32[64]{0:T(128)S(1)} %dynamic-update-slice), channel_id=1, replica_groups=mesh['ep'=32] {'ep'}, use_global_device_ids=true, to_apply=%add | all-reduce | flops 64 | bytes 512
  440.2 0.6 sub.27
  440.8 4.6 %bitcast_reduce_fusion = bf16[8,16,7168]{2,1,0:T(8,128)(2,1)S(1)} fusion(bf16[32,16,7168]{2,1,0:T(8,128)(2,1)} %all-to-all-done.2), kind=kLoop, calls=%fused_computation.6 | loop fusion | flops 2752512 | bytes 9175040 | tf_op jit(solution)/shard_map/reduce_sum | solution.py:81
  445.3 3.0 gather_fusion
  448.3 2.1 fusion.6
  450.4 0.8 copy.46
  (46 shorter events, 2.2 us)
Async XLA Ops:
  0.6 21.8 %copy-start = (bf16[16,7168]{1,0:T(8,128)(2,1)S(1)}, bf16[16,7168]{1,0:T(8,128)(2,1)}, u32[]{:S(2)}) copy-start(bf16[16,7168]{1,0:T(8,128)(2,1)} %param.6) | copy-start | bytes 688132
  2.6 28.6 %all-to-all-start = ((s32[32,1,2]{2,1,0:T(1,128)}), s32[32,1,2]{2,1,0:T(1,128)S(1)}, u32[]{:S(2)}, u32[]{:S(2)}) async-start(s32[32,1,2]{2,1,0:T(1,128)} %bitcast.2), calls=%async_computation | async-start | bytes 32768 | tf_op jit(solution)/shard_map/all_to_all | solution.py:46
  35.3 160.0 %all-to-all-start.1 = ((bf16[32,16,7168]{2,1,0:T(8,128)(2,1)}), bf16[32,16,7168]{2,1,0:T(8,128)(2,1)}, u32[]{:S(2)}, u32[]{:S(2)}) async-start(bf16[32,16,7168]{2,1,0:T(8,128)(2,1)} %bitcast.213), calls=%async_computation.1 | async-start | bytes 14680064 | tf_op jit(solution)/shard_map/all_to_all | solution.py:47
  247.0 11.5 %copy-start.2 = (s32[16,8]{0,1:T(8,128)S(1)}, s32[16,8]{0,1:T(8,128)}, u32[]{:S(2)}) copy-start(s32[16,8]{0,1:T(8,128)} %param.8) | copy-start | bytes 1540
  247.0 11.7 %copy-start.1 = (bf16[7168,16]{0,1:T(8,128)(2,1)S(1)}, bf16[7168,16]{0,1:T(8,128)(2,1)}, u32[]{:S(2)}) copy-start(bf16[7168,16]{0,1:T(8,128)(2,1)} %param.7) | copy-start | bytes 688132
  247.0 193.7 %all-to-all-start.2 = ((bf16[32,16,7168]{2,1,0:T(8,128)(2,1)}), bf16[32,16,7168]{2,1,0:T(8,128)(2,1)}, u32[]{:S(2)}, u32[]{:S(2)}) async-start(bf16[32,16,7168]{2,1,0:T(8,128)(2,1)} %select_convert_fusion), calls=%async_computation.2 | async-start | bytes 14680064 | tf_op jit(solution)/shard_map/all_to_all | solution.py:74
where the time goes:
time: 452 us; the launch traced here: 451 us
  blocking collectives  179 us (40%)
  waiting for transfers between devices  154 us (34%)
  local copies, waits for them, and re-layouts  33.7 us (7%)
  matrix products  30.3 us (7%)
  other arithmetic  28.6 us (6%)
  starting transfers between devices  25 us (6%)
    unnamed x1, blocking collectives  179 us
    all_to_all x1, waiting for transfers between devices, per_device(): lax.all_to_all(send_rows, 'ep', split_axis=0, concat_axis=0, tiled=True)  154 us
    convert_element_type x1, other arithmetic, per_device(): result.reshape(device_count, capacity, features).astype(jnp.bfloat16)  13.3 us
    all_to_all x1, starting transfers between devices, per_device(): lax.all_to_all(result.reshape(device_count, capacity, features).astype(jn...  11.5 us
    dot_general x1, matrix products, per_device(): jnp.einsum('erf,efd->erd', hidden, down_proj[0], preferred_element_type=j...  10.5 us
    slice x1, local copies, waits for them, and re-layouts, per_device(): produced[slot_expert]  10.4 us
    select_n x1, other arithmetic, per_device(): group_rows = jnp.zeros((group_count * capacity, features), tokens.dtype)....  9.95 us
    dot_general x1, matrix products, per_device(): jnp.einsum('rd,edf->erf', arrived_rows, up_proj[0], preferred_element_typ...  9.2 us
  transfers between devices with their start and end apart: 3, of which 1 were waited for; matrix products, arithmetic and copies ran while one was open for 5% of the time, Pallas kernels for 0%

commit v1 on v0

v1 whole, which is shorter than its diff:
```python
import jax
import jax.numpy as jnp
from jax import lax
from jax.sharding import PartitionSpec as P

SPLIT = 4


route_scale = 2.5


def per_device(tokens, router_weight, expert_ids, gate_proj, up_proj, down_proj):
    experts = router_weight.shape[1]
    held = gate_proj.shape[1]
    fanout = expert_ids.shape[1]
    features = tokens.shape[1]
    logits = jnp.dot(tokens, router_weight, preferred_element_type=jnp.float32)
    scores = jax.nn.sigmoid(logits)
    hits = expert_ids[:, :, None] == jnp.arange(experts, dtype=jnp.int32)
    picked = jnp.sum(jnp.where(hits, scores[:, None, :], 0.0), axis=2)
    gates = route_scale * picked / jnp.sum(picked, axis=1, keepdims=True)
    dense = jnp.sum(jnp.where(hits, gates[:, :, None], 0.0), axis=1)
    named = jnp.sum(hits.astype(jnp.float32), axis=1)
    small = lax.all_gather(jnp.concatenate([dense, named], axis=1), "ep", axis=0, tiled=True)
    rows = lax.all_gather(tokens, "ep", axis=0, tiled=True)
    load = jnp.sum(small[:, experts:], axis=0)
    load_excess = load - float(small.shape[0] * fanout // experts)
    group = lax.axis_index("ep") // SPLIT
    weights = lax.dynamic_slice_in_dim(small, group * held, held, axis=1)
    parts = []
    for slot in range(held):
        gate_act = jnp.dot(rows, gate_proj[0, slot], preferred_element_type=jnp.float32)
        up_act = jnp.dot(rows, up_proj[0, slot], preferred_element_type=jnp.float32)
        hidden = jax.nn.silu(gate_act) * up_act * weights[:, slot : slot + 1]
        parts.append(hidden.astype(jnp.bfloat16))
    hidden = jnp.concatenate(parts, axis=1)
    down = down_proj[0].reshape(-1, features)
    partial = jnp.dot(hidden, down, preferred_element_type=jnp.float32).astype(jnp.bfloat16)
    mixed = lax.psum_scatter(partial, "ep", scatter_dimension=0, tiled=True)
    return mixed, load_excess


def solution(mesh):
    in_specs = (
        P("ep", None),
        P(),
        P("ep", None),
        P("ep", None, None, None),
        P("ep", None, None, None),
        P("ep", None, None, None),
    )
    out_specs = (P("ep", None), P())
    return jax.shard_map(
        per_device, mesh=mesh, in_specs=in_specs, out_specs=out_specs, check_vma=False
    )
```

time: 452 us -> 268 us (0.59)
  blocking collectives: 179 us -> 44.4 us
  local copies, waits for them, and re-layouts: 33.7 us -> 1.17 us
  other arithmetic: 28.6 us -> 1.26 us
  starting transfers between devices: 25 us -> 0.08 us
  waiting for transfers between devices: 154 us -> 178 us
  between operations: 0.9 us -> 14.2 us
    unnamed x1 -> x0, blocking collectives: 179 us -> none
    all_to_all x3 -> x0, waiting for transfers between devices: 154 us -> none  [the longest x1 154 us: per_device(): lax.all_to_all(send_rows, 'ep', split_axis=0, concat_axis=0, tiled=True)]
    reduce_scatter x0 -> x1, waiting for transfers between devices: none -> 146 us  [per_device(): mixed = lax.psum_scatter(partial, 'ep', scatter_dimension=0, tiled=True)]
    all_gather x0 -> x1, blocking collectives: none -> 44.4 us  [per_device(): lax.all_gather(jnp.concatenate([dense, named], axis=1), 'ep', axis=0, til...]
    all_gather x0 -> x1, waiting for transfers between devices: none -> 32 us  [per_device(): rows = lax.all_gather(tokens, 'ep', axis=0, tiled=True)]
    all_to_all x3 -> x0, starting transfers between devices: 25 us -> none  [the longest x1 11.5 us: per_device(): lax.all_to_all(result.reshape(device_count, capacity, features).astype(jn...]
    convert_element_type x2 -> x0, other arithmetic: 13.4 us -> none  [the longest x1 13.3 us: per_device(): result.reshape(device_count, capacity, features).astype(jnp.bfloat16)]
    slice x1, local copies, waits for them, and re-layouts: 10.4 us -> 0.37 us  [per_device(): hidden = jax.nn.silu(gate_act) * up_act * weights[:, slot:slot + 1]]
  transfers between devices with their start and end apart: 3 -> 2, of which waited for: 1 -> 2; matrix products, arithmetic and copies ran while one was open for 5% -> 1% of each run, Pallas kernels for 0% -> 0%
where the time goes in v1:
time: 268 us
  waiting for transfers between devices  178 us (66%)
  blocking collectives  44.4 us (17%)
  matrix products  28.9 us (11%)
  between operations  14.2 us (5%)
    reduce_scatter x1, waiting for transfers between devices, per_device(): mixed = lax.psum_scatter(partial, 'ep', scatter_dimension=0, tiled=True)  146 us
    all_gather x1, blocking collectives, per_device(): lax.all_gather(jnp.concatenate([dense, named], axis=1), 'ep', axis=0, til...  44.4 us
    all_gather x1, waiting for transfers between devices, per_device(): rows = lax.all_gather(tokens, 'ep', axis=0, tiled=True)  32 us
    dot_general x2, matrix products, per_device(): up_act = jnp.dot(rows, up_proj[0, slot], preferred_element_type=jnp.float32)  10.8 us
    dot_general x2, matrix products, per_device(): jnp.dot(rows, gate_proj[0, slot], preferred_element_type=jnp.float32)  10.7 us
    dot_general x1, matrix products, per_device(): jnp.dot(hidden, down, preferred_element_type=jnp.float32)  6.19 us
  transfers between devices with their start and end apart: 2, of which 2 were waited for; matrix products, arithmetic and copies ran while one was open for 1% of the time, Pallas kernels for 0%

profile of v1, /device:TPU:0, one launch (start us, length us, event | category | flops | bytes accessed | tf_op | source)
XLA Modules:
  0.0 268.2 jit_solution(15128973468916054226)
XLA Ops:
  7.2 0.0 copy-start
  7.2 0.0 all-gather.2.cloned.1.call-start
  7.2 0.7 all-gather.2.cloned.1.call-update
  7.9 0.0 reduce-scatter.2.cloned.1.call-start
  8.0 0.8 copy.11
  8.7 1.1 fusion.32
  9.9 0.3 select_reduce_fusion
  10.2 0.1 multiply_divide_fusion
  10.3 0.1 select_reduce_fusion.2
  10.4 0.1 pad_maximum_fusion
  10.5 44.4 %all_gather.7 = f32[512,32]{1,0:T(8,128)S(1)} all-gather(f32[16,32]{1,0:T(8,128)S(1)} %pad_maximum_fusion), channel_id=1, replica_groups=mesh['ep'=32] {'ep'}, dimensions={0}, use_global_device_ids=true | all-gather | bytes 67584 | tf_op jit(solution)/shard_map/all_gather | solution.py:24
  54.9 0.4 dynamic-slice_reduce_fusion.1
  55.3 32.0 %all-gather.2.cloned.1.call-done = bf16[512,7168]{1,0:T(8,128)(2,1)} async-done(((bf16[16,7168]{1,0:T(8,128)(2,1)}), bf16[512,7168]{1,0:T(8,128)(2,1)}) %all-gather.2.cloned.1.call-update) | async-done | bytes 7340048 | tf_op jit(solution)/shard_map/all_gather | solution.py:25
  87.2 6.4 %fusion.2 = f32[512,256]{0,1:T(8,128)S(1)} fusion(bf16[512,7168]{1,0:T(8,128)(2,1)} %all-gather.2.cloned.1.call-done, bf16[1,2,7168,256]{3,2,1,0:T(8,128)(2,1)} %param.9), kind=kOutput, calls=%fused_computation.3 | convolution fusion | flops 1879048192 | bytes 11534336 | tf_op jit(solution)/shard_map/dot_general | solution.py:32
  93.6 0.0 slice-start.3
  93.6 4.3 %fusion.6 = f32[512,256]{0,1:T(8,128)S(1)} fusion(bf16[512,7168]{1,0:T(8,128)(2,1)S(1)} %copy-done.1, bf16[1,2,7168,256]{3,2,1,0:T(8,128)(2,1)} %param.9), kind=kOutput, calls=%fused_computation.7 | convolution fusion | flops 1879048192 | bytes 11534336 | tf_op jit(solution)/shard_map/dot_general | solution.py:32
  98.0 5.4 %fusion.24 = bf16[512,256]{0,1:T(8,128)(2,1)S(1)} fusion(bf16[512,7168]{1,0:T(8,128)(2,1)} %all-gather.2.cloned.1.call-done, bf16[1,2,7168,256]{3,2,1,0:T(8,128)(2,1)S(1)} %bitcast.36, f32[512,256]{0,1:T(8,128)S(1)} %fusion.2, f32[512]{0:T(512)S(1)} %get-tuple-element.3), kind=kOutput, calls=%fused_computation.17 | convolution fusion | flops 1879965696 | bytes 11798528 | tf_op jit(solution)/shard_map/dot_general | solution.py:33
  103.5 0.0 slice-start.1
  103.5 5.4 %fusion.27 = bf16[512,256]{0,1:T(8,128)(2,1)S(1)} fusion(bf16[512,7168]{1,0:T(8,128)(2,1)} %all-gather.2.cloned.1.call-done, bf16[1,2,7168,256]{3,2,1,0:T(8,128)(2,1)S(1)} %bitcast.36, f32[512,256]{0,1:T(8,128)S(1)} %fusion.6, f32[512]{0:T(512)S(1)} %get-tuple-element.2), kind=kOutput, calls=%fused_computation.18 | convolution fusion | flops 1879965696 | bytes 11798528 | tf_op jit(solution)/shard_map/dot_general | solution.py:33
  108.9 6.2 %convolution_convert_fusion = bf16[512,7168]{1,0:T(8,128)(2,1)} fusion(bf16[512,7168]{1,0:T(8,128)(2,1)S(1)} %bitcast.34, bf16[512,256]{0,1:T(8,128)(2,1)S(1)} %fusion.24, bf16[512,256]{0,1:T(8,128)(2,1)S(1)} %fusion.27), kind=kOutput, calls=%fused_computation | convolution fusion | flops 3762814976 | bytes 15204352 | tf_op jit(solution)/shard_map/dot_general | solution.py:38
  115.1 0.0 reduce-scatter.2.cloned.1.call-update
  115.1 0.1 slice_reduce_fusion
  115.3 0.5 broadcast_add_fusion
  115.8 145.6 %reduce-scatter.2.cloned.1.call-done = bf16[16,7168]{1,0:T(8,128)(2,1)} async-done(((bf16[512,7168]{1,0:T(8,128)(2,1)}), bf16[16,7168]{1,0:T(8,128)(2,1)}) %reduce-scatter.2.cloned.1.call-update) | async-done | bytes 229392 | tf_op jit(solution)/shard_map/reduce_scatter | solution.py:39
  (11 shorter events, 0.0 us)
Async XLA Ops:
  7.2 1.6 copy-start
  7.2 80.0 %all-gather.2.cloned.1.call-start = ((), (), s32[]{:S(2)}) async-start(), calls=%async_computation.1 | async-start | bytes 7569408 | tf_op jit(solution)/shard_map/all_gather | solution.py:25
  7.9 253.4 %reduce-scatter.2.cloned.1.call-start = ((), (), s32[]{:S(2)}) async-start(), calls=%async_computation.2 | async-start | bytes 7569408 | tf_op jit(solution)/shard_map/reduce_scatter | solution.py:39
  87.2 6.4 %copy-start.1 = (bf16[512,7168]{1,0:T(8,128)(2,1)S(1)}, bf16[512,7168]{1,0:T(8,128)(2,1)}, u32[]{:S(2)}) copy-start(bf16[512,7168]{1,0:T(8,128)(2,1)} %all-gather.2.cloned.1.call-done) | copy-start | bytes 22020100
  87.2 10.8 %slice-start.2 = ((s8[7340032]{0:T(1024)(128)(4,1)}), s8[4194304]{0:T(1024)(128)(4,1)S(1)}, s32[]{:S(2)}) async-start(s8[7340032]{0:T(1024)(128)(4,1)} %bitcast.35), calls=%async_computation.5 | async-start | bytes 8388608
  93.6 4.4 %slice-start.3 = ((s8[7340032]{0:T(1024)(128)(4,1)}), s8[3145728]{0:T(1024)(128)(4,1)S(1)}, s32[]{:S(2)}) async-start(s8[7340032]{0:T(1024)(128)(4,1)} %bitcast.35), calls=%async_computation.6 | async-start | bytes 6291456
  98.0 10.9 %slice-start = ((s8[7340032]{0:T(1024)(128)(4,1)}), s8[4194304]{0:T(1024)(128)(4,1)S(1)}, s32[]{:S(2)}) async-start(s8[7340032]{0:T(1024)(128)(4,1)} %bitcast.32), calls=%async_computation.3 | async-start | bytes 8388608
  103.5 5.4 %slice-start.1 = ((s8[7340032]{0:T(1024)(128)(4,1)}), s8[3145728]{0:T(1024)(128)(4,1)S(1)}, s32[]{:S(2)}) async-start(s8[7340032]{0:T(1024)(128)(4,1)} %bitcast.32), calls=%async_computation.4 | async-start | bytes 6291456
Sparse Core Ops, SparseCore 0:
  10.8 76.3 all-gather.1
  115.2 146.0 reduce-scatter.1

commit v2 on v1

--- a/solution.py
+++ b/solution.py
@@ -1,12 +1,352 @@
+import functools
+
 import jax
 import jax.numpy as jnp
 from jax import lax
+from jax.experimental import pallas as pl
+from jax.experimental.pallas import tpu as pltpu
 from jax.sharding import PartitionSpec as P
 
 SPLIT = 4
+MESH = pl.DeviceIdType.MESH
+LANES = 128
+VMEM_LIMIT = 67_000_000
 
 
 route_scale = 2.5
+
+
+def kernel(
+    chunk,
+    tok_hbm, small_hbm, gate_hbm, up_hbm, down_hbm,
+    out_ref, load_ref,
+    rows, small, wg, wu, wd, acc_g, acc_u, hid, part,
+    r0, q0, r1, q1, r2, q2, r3,
+    send, recv, ssend, srecv, local,
+):
+    deep = rows.shape[0]
+    tok = rows.shape[4]
+    features = rows.shape[5]
+    held = wg.shape[0]
+    ff = wg.shape[2]
+    total_rows = deep * 8 * tok
+    pair = 2 * chunk
+    count = features // pair
+    me = lax.axis_index("ep")
+    core = lax.rem(me, 2)
+    x = lax.rem(me // 2, 2)
+    y = lax.rem(me // 4, 2)
+    z = me // 8
+
+    def index(zi, yi, xi, ci):
+        return ((zi * 2 + yi) * 2 + xi) * 2 + ci
+
+    core_peer = index(z, y, x, 1 - core)
+    x_peer = index(z, y, 1 - x, core)
+    y_peer = index(z, 1 - y, x, core)
+    z_at = [lax.rem(z + o, deep) for o in range(1, deep)]
+    z_peers = [index(zi, y, x, core) for zi in z_at]
+    hops = deep - 1
+
+    fetch = [
+        pltpu.make_async_copy(tok_hbm, rows.at[z, y, x, core], local.at[0]),
+        pltpu.make_async_copy(small_hbm, small.at[z, y, x, core], local.at[1]),
+        pltpu.make_async_copy(gate_hbm.at[0], wg, local.at[2]),
+        pltpu.make_async_copy(up_hbm.at[0], wu, local.at[3]),
+        pltpu.make_async_copy(down_hbm.at[0], wd, local.at[4]),
+    ]
+    for copy in fetch:
+        copy.start()
+
+    barrier = pltpu.get_barrier_semaphore()
+    peers = [core_peer, x_peer, y_peer] + z_peers
+    for peer in peers:
+        pl.semaphore_signal(barrier, inc=1, device_id=(peer,), device_id_type=MESH)
+    pl.semaphore_wait(barrier, len(peers))
+
+    def remote(src, dst, ss, rs, peer):
+        return pltpu.make_async_remote_copy(
+            src_ref=src, dst_ref=dst, send_sem=ss, recv_sem=rs,
+            device_id=(peer,), device_id_type=MESH,
+        )
+
+    def span(p):
+        return pl.ds(pl.multiple_of(p * pair, pair), pair)
+
+    def span_a(p):
+        return pl.ds(pl.multiple_of(p * pair, chunk), chunk)
+
+    def span_b(p):
+        return pl.ds(pl.multiple_of(p * pair + chunk, chunk), chunk)
+
+    def put(p, slot, src, dst, peer):
+        return remote(src, dst, send.at[p, slot], recv.at[p, slot], peer)
+
+    def same(ref, at, p, slot, peer):
+        view = ref.at[at]
+        return put(p, slot, view, view, peer)
+
+    every = slice(None)
+
+    def gather_z(p):
+        return [
+            same(rows, (z, y, x, core, every, span(p)), p, o, z_peers[o]) for o in range(hops)
+        ]
+
+    def gather_1(p):
+        return [
+            same(rows, (every, y, x, core, every, span_a(p)), p, hops, x_peer),
+            same(rows, (every, y, x, core, every, span_b(p)), p, hops + 1, y_peer),
+        ]
+
+    def gather_2(p):
+        return [
+            same(rows, (every, y, every, core, every, span_a(p)), p, hops + 2, y_peer),
+            same(rows, (every, every, x, core, every, span_b(p)), p, hops + 3, x_peer),
+        ]
+
+    def gather_core(p):
+        return [
+            same(rows, (every, every, every, core, every, span(p)), p, hops + 4, core_peer)
+        ]
+
+    def small_copy(at, slot, peer):
+        view = small.at[at]
+        return remote(view, view, ssend.at[slot], srecv.at[slot], peer)
+
+    small_z = [small_copy((z, y, x, core), o, z_peers[o]) for o in range(hops)]
+    small_x = [small_copy((every, y, x, core), hops, x_peer)]
+    small_y = [small_copy((every, y, every, core), hops + 1, y_peer)]
+    small_core = [small_copy((every, every, every, core), hops + 2, core_peer)]
+
+    def start(copies):
+        for copy in copies:
+            copy.start()
+
+    def wait(copies):
+        for copy in copies:
+            copy.wait()
+
+    fetch[0].wait()
+    fetch[1].wait()
+
+    def first(p, carry):
+        start(gather_z(p))
+        return carry
+
+    start(gather_z(0))
+    start(small_z)
+    lax.fori_loop(1, count, first, 0)
+    acc_g[...] = jnp.zeros_like(acc_g)
+    acc_u[...] = jnp.zeros_like(acc_u)
+    fetch[2].wait()
+    fetch[3].wait()
+
+    def gather_step(t, carry):
+        @pl.when(t < count)
+        def _():
+            wait(gather_z(t))
+            start(gather_1(t))
+
+        @pl.when(jnp.logical_and(t >= 1, t < count + 1))
+        def _():
+            wait(gather_1(t - 1))
+            start(gather_2(t - 1))
+
+        @pl.when(jnp.logical_and(t >= 2, t < count + 2))
+        def _():
+            wait(gather_2(t - 2))
+            start(gather_core(t - 2))
+
+        @pl.when(t >= 3)
+        def _():
+            p = t - 3
+            wait(gather_core(p))
+            block = rows[:, :, :, :, :, span(p)].reshape(total_rows, pair)
+            for slot in range(held):
+                acc_g[slot] += jnp.dot(
+                    block, wg[slot, span(p), :], preferred_element_type=jnp.float32
+                )
+                acc_u[slot] += jnp.dot(
+                    block, wu[slot, span(p), :], preferred_element_type=jnp.float32
+                )
+
+        @pl.when(t == 0)
+        def _():
+            wait(small_z)
+            start(small_x)
+
+        @pl.when(t == 1)
+        def _():
+            wait(small_x)
+            start(small_y)
+
+        @pl.when(t == 2)
+        def _():
+            wait(small_y)
+            start(small_core)
+
+        return carry
+
+    lax.fori_loop(0, count + 3, gather_step, 0)
+    wait(small_core)
+    fetch[4].wait()
+
+    table = small[...].reshape(total_rows, LANES)
+    load_ref[...] = jnp.broadcast_to(jnp.sum(table, axis=0, keepdims=True), load_ref.shape)
+    lane = lax.broadcasted_iota(jnp.int32, (total_rows, LANES), 1)
+    for slot in range(held):
+        mine = lane == me // SPLIT * held + slot
+        weight = jnp.sum(jnp.where(mine, table, 0.0), axis=1, keepdims=True)
+        gate_act = acc_g[slot]
+        hidden = gate_act / (1.0 + jnp.exp(-gate_act)) * acc_u[slot] * weight
+        hid[:, slot * ff : (slot + 1) * ff] = hidden.astype(hid.dtype)
+
+    base = hops + 5
+
+    def fold_core(p):
+        return [
+            put(p, base, part.at[:, :, :, 1 - core, :, span(p)], r0.at[:, :, :, :, span(p)], core_peer)
+        ]
+
+    def fold_1(p):
+        a, b = span_a(p), span_b(p)
+        return [
+            put(p, base + 1, q0.at[:, 1 - y, :, :, a], r1.at[:, :, :, a], y_peer),
+            put(p, base + 2, q0.at[:, :, 1 - x, :, b], r1.at[:, :, :, b], x_peer),
+        ]
+
+    def fold_2(p):
+        a, b = span_a(p), span_b(p)
+        return [
+            put(p, base + 3, q1.at[:, 1 - x, :, a], r2.at[:, :, a], x_peer),
+            put(p, base + 4, q1.at[:, 1 - y, :, b], r2.at[:, :, b], y_peer),
+        ]
+
+    def fold_z(p):
+        return [
+            put(p, base + 5 + o, q2.at[z_at[o], :, span(p)], r3.at[o, :, span(p)], z_peers[o])
+            for o in range(hops)
+        ]
+
+    def add(a, b):
+        return (a.astype(jnp.float32) + b.astype(jnp.float32)).astype(jnp.bfloat16)
+
+    def fold_step(t, carry):
+        @pl.when(t < count)
+        def _():
+            s = span(t)
+            down = wd[:, :, s].reshape(held * ff, pair)
+            made = jnp.dot(hid[...], down, preferred_element_type=jnp.float32)
+            part[:, :, :, :, :, s] = made.astype(jnp.bfloat16).reshape(
+                deep, 2, 2, 2, tok, pair
+            )
+            start(fold_core(t))
+
+        @pl.when(jnp.logical_and(t >= 1, t < count + 1))
+        def _():
+            p = t - 1
+            s = span(p)
+            wait(fold_core(p))
+            q0[:, :, :, :, s] = add(part[:, :, :, core, :, s], r0[:, :, :, :, s])
+            start(fold_1(p))
+
+        @pl.when(jnp.logical_and(t >= 2, t < count + 2))
+        def _():
+            p = t - 2
+            a, b = span_a(p), span_b(p)
+            wait(fold_1(p))
+            q1[:, :, :, a] = add(q0[:, y, :, :, a], r1[:, :, :, a])
+            q1[:, :, :, b] = add(q0[:, :, x, :, b], r1[:, :, :, b])
+            start(fold_2(p))
+
+        @pl.when(jnp.logical_and(t >= 3, t < count + 3))
+        def _():
+            p = t - 3
+            a, b = span_a(p), span_b(p)
+            wait(fold_2(p))
+            q2[:, :, a] = add(q1[:, x, :, a], r2[:, :, a])
+            q2[:, :, b] = add(q1[:, y, :, b], r2[:, :, b])
+            start(fold_z(p))
+
+        @pl.when(t >= 4)
+        def _():
+            p = t - 4
+            s = span(p)
+            wait(fold_z(p))
+            total = q2[z, :, s].astype(jnp.float32)
+            for o in range(hops):
+                total = total + r3[o, :, s].astype(jnp.float32)
+            out_ref[:, s] = total.astype(out_ref.dtype)
+
+        return carry
+
+    lax.fori_loop(0, count + 4, fold_step, 0)
+
+
+def exchange(tokens, small, gate_proj, up_proj, down_proj, devices, chunk):
+    tok, features = tokens.shape
+    held, _, ff = gate_proj.shape[1:]
+    deep = devices // 8
+    total_rows = devices * tok
+    count = features // (2 * chunk)
+    hops = deep - 1
+    slots = 2 * (hops + 5)
+    bf16, f32 = jnp.bfloat16, jnp.float32
+    hbm = pl.BlockSpec(memory_space=pl.ANY)
+    vmem = pl.BlockSpec(memory_space=pltpu.VMEM)
+    return pl.pallas_call(
+        functools.partial(kernel, chunk),
+        out_shape=(
+            jax.ShapeDtypeStruct((tok, features), bf16),
+            jax.ShapeDtypeStruct((8, LANES), f32),
+        ),
+        in_specs=[hbm] * 5,
+        out_specs=(vmem, vmem),
+        scratch_shapes=[
+            pltpu.VMEM((deep, 2, 2, 2, tok, features), bf16),
+            pltpu.VMEM((deep, 2, 2, 2, tok, LANES), f32),
+            pltpu.VMEM((held, features, ff), bf16),
+            pltpu.VMEM((held, features, ff), bf16),
+            pltpu.VMEM((held, ff, features), bf16),
+            pltpu.VMEM((held, total_rows, ff), f32),
+            pltpu.VMEM((held, total_rows, ff), f32),
+            pltpu.VMEM((total_rows, held * ff), bf16),
+            pltpu.VMEM((deep, 2, 2, 2, tok, features), bf16),
+            pltpu.VMEM((deep, 2, 2, tok, features), bf16),
+            pltpu.VMEM((deep, 2, 2, tok, features), bf16),
+            pltpu.VMEM((deep, 2, tok, features), bf16),
+            pltpu.VMEM((deep, 2, tok, features), bf16),
+            pltpu.VMEM((deep, tok, features), bf16),
+            pltpu.VMEM((deep, tok, features), bf16),
+            pltpu.VMEM((max(hops, 1), tok, features), bf16),
+            pltpu.SemaphoreType.DMA((count, slots)),
+            pltpu.SemaphoreType.DMA((count, slots)),
+            pltpu.SemaphoreType.DMA((hops + 3,)),
+            pltpu.SemaphoreType.DMA((hops + 3,)),
+            pltpu.SemaphoreType.DMA((5,)),
+        ],
+        compiler_params=pltpu.CompilerParams(
+            collective_id=0, has_side_effects=True, vmem_limit_bytes=VMEM_LIMIT
+        ),
+    )(tokens, small, gate_proj, up_proj, down_proj)
+
+
+def chunk_width(devices, tokens, expert_ids, router_weight, gate_proj):
+    tok, features = tokens.shape
+    held, _, ff = gate_proj.shape[1:]
+    row_bytes = devices * tok * features * 2
+    need = 4 * row_bytes + 3 * held * features * ff * 2 + devices * tok * held * ff * 10
+    fits = need + (2 << 20) <= VMEM_LIMIT and 2 * router_weight.shape[1] <= LANES
+    if devices % 8 or tok % 16 or ff % LANES or not fits:
+        return 0
+    for width in (CHUNK, 2 * LANES, LANES):
+        if features % (2 * width) == 0:
+            return width
+    return 0
+
+
+CHUNK = 512
 
 
 def per_device(tokens, router_weight, expert_ids, gate_proj, up_proj, down_proj):
@@ -21,10 +361,20 @@
     gates = route_scale * picked / jnp.sum(picked, axis=1, keepdims=True)
     dense = jnp.sum(jnp.where(hits, gates[:, :, None], 0.0), axis=1)
     named = jnp.sum(hits.astype(jnp.float32), axis=1)
-    small = lax.all_gather(jnp.concatenate([dense, named], axis=1), "ep", axis=0, tiled=True)
+    devices = lax.axis_size("ep")
+    chunk = chunk_width(devices, tokens, expert_ids, router_weight, gate_proj)
+    mean_load = float(devices * tokens.shape[0] * fanout // experts)
+    both = jnp.concatenate([dense, named], axis=1)
+    if chunk:
+        both = jnp.pad(both, ((0, 0), (0, LANES - 2 * experts)))
+        mixed, loads = exchange(
+            tokens, both, gate_proj, up_proj, down_proj, devices, chunk
+        )
+        return mixed, loads[0, experts : 2 * experts] - mean_load
+    small = lax.all_gather(both, "ep", axis=0, tiled=True)
     rows = lax.all_gather(tokens, "ep", axis=0, tiled=True)
     load = jnp.sum(small[:, experts:], axis=0)
-    load_excess = load - float(small.shape[0] * fanout // experts)
+    load_excess = load - mean_load
     group = lax.axis_index("ep") // SPLIT
     weights = lax.dynamic_slice_in_dim(small, group * held, held, axis=1)
     parts = []

time: 268 us -> 98.4 us (0.37)
  waiting for transfers between devices: 178 us -> 0 us
  Pallas kernels: 0 us -> 91.4 us
  blocking collectives: 44.4 us -> 0 us
  matrix products: 28.9 us -> 1.25 us
  between operations: 14.2 us -> 0.67 us
    reduce_scatter x1 -> x0, waiting for transfers between devices: 146 us -> none  [per_device(): mixed = lax.psum_scatter(partial, 'ep', scatter_dimension=0, tiled=True)]
    pallas_call x0 -> x1, Pallas kernels: none -> 91.4 us  [exchange(): pl.pallas_call(functools.partial(kernel, chunk), out_shape=(jax.ShapeDtyp...]
    all_gather x1 -> x0, blocking collectives: 44.4 us -> none  [per_device(): lax.all_gather(jnp.concatenate([dense, named], axis=1), 'ep', axis=0, til...]
    all_gather x1 -> x0, waiting for transfers between devices: 32 us -> none  [per_device(): rows = lax.all_gather(tokens, 'ep', axis=0, tiled=True)]
    dot_general x5 -> x0, matrix products: 27.7 us -> none  [the longest x2 10.8 us: per_device(): up_act = jnp.dot(rows, up_proj[0, slot], preferred_element_type=jnp.float32)]
  transfers between devices with their start and end apart: 2 -> 0, of which waited for: 2 -> 0; matrix products, arithmetic and copies ran while one was open for 1% -> 0% of each run, Pallas kernels for 0% -> 0%
where the time goes in v2:
time: 98.4 us; the launch traced here: 98.2 us
  Pallas kernels  91.4 us (93%)
  other arithmetic  2.43 us (2%)
  local copies, waits for them, and re-layouts  2.4 us (2%)
  matrix products  1.25 us (1%)
    pallas_call x1, Pallas kernels, exchange(): pl.pallas_call(functools.partial(kernel, chunk), out_shape=(jax.ShapeDtyp...  91.4 us
    unnamed x2, local copies, waits for them, and re-layouts  2.4 us

profile of v2, /device:TPU:0, one launch (start us, length us, event | category | flops | bytes accessed | tf_op | source)
XLA Modules:
  0.0 98.2 jit_solution(6403107298631734233)
XLA Ops:
  0.6 0.8 copy.9
  1.4 1.3 %fusion.2 = f32[16,16]{1,0:T(8,128)S(1)} fusion(bf16[16,7168]{1,0:T(8,128)(2,1)} %tok_hbm.1, bf16[7168,16]{0,1:T(8,128)(2,1)} %param.7), kind=kOutput, calls=%fused_computation.3 | convolution fusion | flops 3670784 | bytes 459776 | tf_op jit(solution)/shard_map/dot_general | solution.py:357
  2.7 0.3 select_reduce_fusion
  3.0 0.1 multiply_divide_fusion
  3.0 0.1 select_reduce_fusion.2
  3.2 0.7 select_maximum_fusion.small_hbm
  3.8 91.4 %shard_map.77 = (bf16[16,7168]{1,0:T(8,128)(2,1)}, f32[8,128]{1,0:T(8,128)}) custom-call(bf16[16,7168]{1,0:T(8,128)(2,1)} %tok_hbm.1, f32[16,128]{1,0:T(8,128)} %select_maximum_fusion.small_hbm, bf16[1,2,7168,256]{3,2,1,0:T(8,128)(2,1)} %gate_hbm.1, bf16[1,2,7168,256]{3,2,1,0:T(8,128)(2,1)} %up_hbm.1, bf16[1,2,256,7168]{3,2,1,0:T(8,128)(2,1)} %down_hbm.1), custom_call_target="tpu_custom_call" | custom-call | tf_op jit(solution)/shard_map/pallas_call | solution.py:298
  95.3 1.3 %add_bitcast_fusion = f32[16]{0:T(128)} fusion(f32[8,128]{1,0:T(8,128)} %get-tuple-element.5), kind=kLoop, calls=%fused_computation.12 | loop fusion | flops 16 | bytes 128 | tf_op jit(solution)/shard_map/sub | solution.py:373
  96.5 1.6 %copy.11 = bf16[16,7168]{1,0:T(8,128)(2,1)} copy(bf16[16,7168]{1,0:T(8,128)(2,1)} %get-tuple-element.12) | data formatting | bytes 458752

commit v3 on v2

--- a/solution.py
+++ b/solution.py
@@ -17,7 +17,7 @@
 
 
 def kernel(
-    chunk,
+    chunk, mean_load,
     tok_hbm, small_hbm, gate_hbm, up_hbm, down_hbm,
     out_ref, load_ref,
     rows, small, wg, wu, wd, acc_g, acc_u, hid, part,
@@ -139,8 +139,6 @@
     lax.fori_loop(1, count, first, 0)
     acc_g[...] = jnp.zeros_like(acc_g)
     acc_u[...] = jnp.zeros_like(acc_u)
-    fetch[2].wait()
-    fetch[3].wait()
 
     def gather_step(t, carry):
         @pl.when(t < count)
@@ -161,6 +159,12 @@
         @pl.when(t >= 3)
         def _():
             p = t - 3
+
+            @pl.when(p == 0)
+            def _():
+                fetch[2].wait()
+                fetch[3].wait()
+
             wait(gather_core(p))
             block = rows[:, :, :, :, :, span(p)].reshape(total_rows, pair)
             for slot in range(held):
@@ -193,10 +197,11 @@
     fetch[4].wait()
 
     table = small[...].reshape(total_rows, LANES)
-    load_ref[...] = jnp.broadcast_to(jnp.sum(table, axis=0, keepdims=True), load_ref.shape)
+    experts = load_ref.shape[1]
+    load_ref[...] = jnp.sum(table, axis=0, keepdims=True)[:, :experts] - mean_load
     lane = lax.broadcasted_iota(jnp.int32, (total_rows, LANES), 1)
     for slot in range(held):
-        mine = lane == me // SPLIT * held + slot
+        mine = lane == load_ref.shape[1] + me // SPLIT * held + slot
         weight = jnp.sum(jnp.where(mine, table, 0.0), axis=1, keepdims=True)
         gate_act = acc_g[slot]
         hidden = gate_act / (1.0 + jnp.exp(-gate_act)) * acc_u[slot] * weight
@@ -284,7 +289,7 @@
     lax.fori_loop(0, count + 4, fold_step, 0)
 
 
-def exchange(tokens, small, gate_proj, up_proj, down_proj, devices, chunk):
+def exchange(tokens, small, gate_proj, up_proj, down_proj, devices, chunk, mean_load, experts):
     tok, features = tokens.shape
     held, _, ff = gate_proj.shape[1:]
     deep = devices // 8
@@ -296,10 +301,10 @@
     hbm = pl.BlockSpec(memory_space=pl.ANY)
     vmem = pl.BlockSpec(memory_space=pltpu.VMEM)
     return pl.pallas_call(
-        functools.partial(kernel, chunk),
+        functools.partial(kernel, chunk, mean_load),
         out_shape=(
             jax.ShapeDtypeStruct((tok, features), bf16),
-            jax.ShapeDtypeStruct((8, LANES), f32),
+            jax.ShapeDtypeStruct((1, experts), f32),
         ),
         in_specs=[hbm] * 5,
         out_specs=(vmem, vmem),
@@ -366,11 +371,12 @@
     mean_load = float(devices * tokens.shape[0] * fanout // experts)
     both = jnp.concatenate([dense, named], axis=1)
     if chunk:
+        both = jnp.concatenate([named, dense], axis=1)
         both = jnp.pad(both, ((0, 0), (0, LANES - 2 * experts)))
         mixed, loads = exchange(
-            tokens, both, gate_proj, up_proj, down_proj, devices, chunk
+            tokens, both, gate_proj, up_proj, down_proj, devices, chunk, mean_load, experts
         )
-        return mixed, loads[0, experts : 2 * experts] - mean_load
+        return mixed, loads.reshape(-1)
     small = lax.all_gather(both, "ep", axis=0, tiled=True)
     rows = lax.all_gather(tokens, "ep", axis=0, tiled=True)
     load = jnp.sum(small[:, experts:], axis=0)

time: 98.4 us -> 98.2 us (level)
  other arithmetic: 2.43 us -> 1.17 us
  local copies, waits for them, and re-layouts: 2.4 us -> 3.52 us
    sub x1 -> x0, other arithmetic: 1.26 us -> none  [per_device(): return (mixed, loads[0, experts:2 * experts] - mean_load)]
    unnamed x2 -> x3, local copies, waits for them, and re-layouts: 2.4 us -> 3.52 us
where the time goes in v3:
time: 98.2 us; the launch traced here: 98 us
  Pallas kernels  91.4 us (93%)
  local copies, waits for them, and re-layouts  3.52 us (4%)
  matrix products  1.25 us (1%)
  other arithmetic  1.17 us (1%)
    pallas_call x1, Pallas kernels, exchange(): pl.pallas_call(functools.partial(kernel, chunk, mean_load), out_shape=(ja...  91.4 us
    unnamed x3, local copies, waits for them, and re-layouts  3.52 us

profile of v3, /device:TPU:0, one launch (start us, length us, event | category | flops | bytes accessed | tf_op | source)
XLA Modules:
  0.0 98.0 jit_solution(16566259770224415697)
XLA Ops:
  0.6 0.8 copy.9
  1.4 1.3 %fusion.2 = f32[16,16]{1,0:T(8,128)S(1)} fusion(bf16[16,7168]{1,0:T(8,128)(2,1)} %tok_hbm.1, bf16[7168,16]{0,1:T(8,128)(2,1)} %param.7), kind=kOutput, calls=%fused_computation.3 | convolution fusion | flops 3670784 | bytes 459776 | tf_op jit(solution)/shard_map/dot_general | solution.py:362
  2.7 0.3 select_reduce_fusion
  3.0 0.1 multiply_divide_fusion
  3.0 0.1 select_reduce_fusion.2
  3.2 0.7 select_maximum_fusion.small_hbm
  3.8 91.4 %shard_map.77 = (bf16[16,7168]{1,0:T(8,128)(2,1)}, f32[1,16]{1,0:T(1,128)}) custom-call(bf16[16,7168]{1,0:T(8,128)(2,1)} %tok_hbm.1, f32[16,128]{1,0:T(8,128)} %select_maximum_fusion.small_hbm, bf16[1,2,7168,256]{3,2,1,0:T(8,128)(2,1)} %gate_hbm.1, bf16[1,2,7168,256]{3,2,1,0:T(8,128)(2,1)} %up_hbm.1, bf16[1,2,256,7168]{3,2,1,0:T(8,128)(2,1)} %down_hbm.1), custom_call_target="tpu_custom_call" | custom-call | tf_op jit(solution)/shard_map/pallas_call | solution.py:303
  95.3 1.6 %copy.12 = bf16[16,7168]{1,0:T(8,128)(2,1)} copy(bf16[16,7168]{1,0:T(8,128)(2,1)} %get-tuple-element.11) | data formatting | bytes 458752
  96.9 1.1 %copy.13 = f32[16]{0:T(128)} copy(f32[16]{0:T(128)} %bitcast.3) | data formatting | bytes 128
